TPU v7x, 32 devices: a whole 2x2x4 slice. The times are simulated.
32 devices in a mesh: bank: 4 (over x, core), zero: 8 (over z, y).
Axes of the slice: x: 2, y: 2, z: 4, core: 2. Of those that a mesh axis runs over, the one named last changes fastest.
Arguments:
- train_gate: float32 [128, 2048, 768], P('bank', 'zero'), may hold values from -0.1875 to 0.1875
- other_gate: bfloat16 [128, 2048, 768], P('bank', 'zero'), may hold values from -0.0625 to 0.0625
- train_up: float32 [128, 2048, 768], P('bank', 'zero'), may hold values from -0.1875 to 0.1875
- other_up: bfloat16 [128, 2048, 768], P('bank', 'zero'), may hold values from -0.0625 to 0.0625
- router_weight: float32 [2048, 128], P('zero', 'bank'), may hold values from -0.125 to 0.125
- router_gain: float32 [2048], P('zero'), may hold values from 0.25 to 1.75
Outputs:
- ready_gate: bfloat16 [128, 2048, 768], P('bank', None, 'zero')
- ready_up: bfloat16 [128, 2048, 768], P('bank', None, 'zero')
- scale_gate: float32 [128, 768], P('bank', 'zero')
- scale_up: float32 [128, 768], P('bank', 'zero')
- serve_router: bfloat16 [2048, 128], replicated
All inputs are finite; a program needn't handle non-finite values. Where the computation divides by a largest or mean magnitude, that divisor is 1e-20 or more.
Results may differ from a plain program's by a relative error of at most 0.001.
Values may be sent and summed in bfloat16 or wider, within the bound.
A program may use at most 256 MiB of HBM per device.

v0:
```python
import functools

import jax
import jax.numpy as jnp
from jax import lax
from jax.experimental import pallas as pl
from jax.experimental.pallas import tpu as pltpu
from jax.sharding import PartitionSpec as P

LANES = 128
SLOTS = 3


def exchange(
    n, banks, held,
    train_gate, other_gate, train_up, other_up, router,
    ready_gate, ready_up, scale_ref, serve_router,
    train_in, other_in, stage, local_max, peer_max, router_row,
    in_sem, own_sem, send_sem, recv_sem, max_send, max_recv,
    row_send, row_recv, bank_send, bank_recv, router_sem,
):
    trains, others, readies = (train_gate, train_up), (other_gate, other_up), (ready_gate, ready_up)
    experts, rows, width = train_gate.shape
    piece = width // n
    groups = experts // held
    me = lax.axis_index("zero")
    offsets = sorted(range(1, n), key=lambda k: abs(2 * k - n))

    def loads(g):
        slot = lax.rem(g, SLOTS)
        some = pl.ds(g * held, held)
        out = []
        for t in range(2):
            out.append(pltpu.make_async_copy(trains[t].at[some], train_in.at[slot, t], in_sem.at[slot, t, 0]))
            out.append(pltpu.make_async_copy(others[t].at[some], other_in.at[slot, t], in_sem.at[slot, t, 1]))
        return out

    def max_copy(g, k):
        return pltpu.make_async_remote_copy(
            src_ref=local_max.at[g],
            dst_ref=peer_max.at[g, k - 1],
            send_sem=max_send.at[k - 1],
            recv_sem=max_recv.at[g],
            device_id={"zero": lax.rem(me + k, n)},
            device_id_type=pl.DeviceIdType.MESH,
        )

    def find_max(g):
        slot = lax.rem(g, SLOTS)
        for copy in loads(g):
            copy.wait()

        for t in range(2):
            for i in range(held):
                for at in range(0, width, LANES):
                    cols = pl.ds(at, LANES)
                    latest = train_in[slot, t, i, :, cols] + other_in[slot, t, i, :, cols].astype(jnp.float32)
                    local_max[g, t, i:i + 1, cols] = jnp.max(jnp.abs(latest), axis=0, keepdims=True)
        for k in offsets:
            max_copy(g, k).start()

    def mine(ref):
        return ref.at[:, :, pl.ds(pl.multiple_of(me * rows, LANES), rows)]

    def scale_and_send(g):
        slot = lax.rem(g, SLOTS)
        pltpu.make_async_copy(peer_max.at[g], peer_max.at[g], max_recv.at[g]).wait()

        for t in range(2):
            scales = local_max[g, t]
            for k in range(n - 1):
                scales = jnp.maximum(scales, peer_max[g, k, t])
            scale_ref[g, t] = scales
            inverses = 1.0 / scales
            for i in range(held):
                inverse = inverses[i:i + 1, :]
                for at in range(0, width, LANES):
                    cols = pl.ds(at, LANES)
                    latest = train_in[slot, t, i, :, cols] + other_in[slot, t, i, :, cols].astype(jnp.float32)
                    narrow = (latest * inverse[:, at:at + LANES]).astype(jnp.bfloat16)
                    stage[t, g * held + i, cols, :] = narrow.T
        some = pl.ds(g * held, held)
        for k in offsets:
            to = lax.rem(me + k, n)
            for t in range(2):
                pltpu.make_async_remote_copy(
                    src_ref=stage.at[t, some, pl.ds(pl.multiple_of(to * piece, 16), piece), :],
                    dst_ref=mine(readies[t]).at[some],
                    send_sem=send_sem.at[t, k - 1],
                    recv_sem=recv_sem.at[t, k - 1],
                    device_id={"zero": to},
                    device_id_type=pl.DeviceIdType.MESH,
                ).start()
        for t in range(2):
            pltpu.make_async_copy(
                stage.at[t, some, pl.ds(pl.multiple_of(me * piece, 16), piece), :],
                mine(readies[t]).at[some],
                own_sem.at[t],
            ).start()

    bank = lax.axis_index("bank")
    parts = router.shape[0]

    def row_copy(k):
        return pltpu.make_async_remote_copy(
            src_ref=router,
            dst_ref=router_row.at[:, pl.ds(pl.multiple_of(me * rows, LANES), rows)],
            send_sem=row_send.at[k - 1],
            recv_sem=row_recv.at[k - 1],
            device_id={"zero": lax.rem(me + k, n)},
            device_id_type=pl.DeviceIdType.MESH,
        )

    def bank_copy(k):
        return pltpu.make_async_remote_copy(
            src_ref=router_row,
            dst_ref=serve_router.at[pl.ds(pl.multiple_of(bank * parts, 16), parts)],
            send_sem=bank_send.at[k - 1],
            recv_sem=bank_recv.at[k - 1],
            device_id={"bank": lax.rem(bank + k, banks)},
            device_id_type=pl.DeviceIdType.MESH,
        )

    own_row = pltpu.make_async_copy(
        router, router_row.at[:, pl.ds(pl.multiple_of(me * rows, LANES), rows)], router_sem.at[0]
    )
    own_bank = pltpu.make_async_copy(
        router_row, serve_router.at[pl.ds(pl.multiple_of(bank * parts, 16), parts)], router_sem.at[1]
    )

    for g in range(min(SLOTS, groups)):
        for copy in loads(g):
            copy.start()
    barrier = pltpu.get_barrier_semaphore()
    for k in offsets:
        pl.semaphore_signal(
            barrier, inc=1, device_id={"zero": lax.rem(me + k, n)}, device_id_type=pl.DeviceIdType.MESH
        )
    for k in range(1, banks):
        pl.semaphore_signal(
            barrier, inc=1, device_id={"bank": lax.rem(bank + k, banks)}, device_id_type=pl.DeviceIdType.MESH
        )
    own_row.start()
    pl.semaphore_wait(barrier, n + banks - 2)
    for k in offsets:
        row_copy(k).start()
    find_max(0)

    def step(g, carry):
        @pl.when(g + 1 < groups)
        def _():
            find_max(g + 1)

        scale_and_send(g)

        @pl.when(g + SLOTS < groups)
        def _():
            for copy in loads(g + SLOTS):
                copy.start()

        return carry

    lax.fori_loop(0, groups, step, 0)

    own_row.wait()
    for k in offsets:
        row_copy(k).wait()
    own_bank.start()
    for k in range(1, banks):
        bank_copy(k).start()
    own_bank.wait()
    for k in range(1, banks):
        bank_copy(k).wait()

    for k in offsets:
        sent = local_max
        pltpu.make_async_copy(sent, sent, max_send.at[k - 1]).wait()
        to, source = lax.rem(me + k, n), lax.rem(me + n - k, n)
        for t in range(2):
            sent = stage.at[t, :, pl.ds(pl.multiple_of(to * piece, 16), piece), :]
            pltpu.make_async_copy(sent, sent, send_sem.at[t, k - 1]).wait()
            got = readies[t].at[:, :, pl.ds(pl.multiple_of(source * rows, LANES), rows)]
            pltpu.make_async_copy(got, got, recv_sem.at[t, k - 1]).wait()
    for t in range(2):
        pltpu.make_async_copy(mine(readies[t]), mine(readies[t]), own_sem.at[t]).wait()


def by_kernel(n, banks, held, train_gate, other_gate, train_up, other_up, part_router):
    experts, rows, width = train_gate.shape
    piece, groups = width // n, experts // held
    anywhere = pl.BlockSpec(memory_space=pltpu.MemorySpace.HBM)
    ready = jax.ShapeDtypeStruct((experts, piece, n * rows), jnp.bfloat16)
    ready_gate, ready_up, scales, serve_router = pl.pallas_call(
        functools.partial(exchange, n, banks, held),
        out_shape=(
            ready,
            ready,
            jax.ShapeDtypeStruct((groups, 2, held, width), jnp.float32),
            jax.ShapeDtypeStruct((banks * part_router.shape[1], n * rows), jnp.bfloat16),
        ),
        in_specs=[anywhere] * 4 + [pl.BlockSpec(memory_space=pltpu.VMEM)],
        out_specs=(anywhere, anywhere, pl.BlockSpec(memory_space=pltpu.VMEM), anywhere),
        scratch_shapes=[
            pltpu.VMEM((SLOTS, 2, held, rows, width), jnp.float32),
            pltpu.VMEM((SLOTS, 2, held, rows, width), jnp.bfloat16),
            pltpu.VMEM((2, experts, width, rows), jnp.bfloat16),
            pltpu.VMEM((groups, 2, held, width), jnp.float32),
            pltpu.VMEM((groups, n - 1, 2, held, width), jnp.float32),
            pltpu.VMEM((part_router.shape[1], n * rows), jnp.bfloat16),
            pltpu.SemaphoreType.DMA((SLOTS, 2, 2)),
            pltpu.SemaphoreType.DMA((2,)),
            pltpu.SemaphoreType.DMA((2, n - 1)),
            pltpu.SemaphoreType.DMA((2, n - 1)),
            pltpu.SemaphoreType.DMA((n - 1,)),
            pltpu.SemaphoreType.DMA((groups,)),
            pltpu.SemaphoreType.DMA((n - 1,)),
            pltpu.SemaphoreType.DMA((n - 1,)),
            pltpu.SemaphoreType.DMA((banks - 1,)),
            pltpu.SemaphoreType.DMA((banks - 1,)),
            pltpu.SemaphoreType.DMA((2,)),
        ],
        compiler_params=pltpu.CompilerParams(
            collective_id=0, has_side_effects=True, vmem_limit_bytes=56 * 2**20
        ),
    )(train_gate, other_gate, train_up, other_up, part_router.T)
    mine = lax.dynamic_slice_in_dim(scales, lax.axis_index("zero") * piece, piece, axis=3)
    mine = jnp.swapaxes(mine, 0, 1).reshape(2, experts, piece)
    return jnp.swapaxes(ready_gate, 1, 2), jnp.swapaxes(ready_up, 1, 2), mine[0], mine[1], serve_router.T


def by_collectives(train_gate, other_gate, train_up, other_up, part_router):
    latest_gate = train_gate + other_gate.astype(jnp.float32)
    latest_up = train_up + other_up.astype(jnp.float32)
    scale_gate, scale_up = lax.pmax(
        (jnp.max(jnp.abs(latest_gate), axis=1), jnp.max(jnp.abs(latest_up), axis=1)), "zero"
    )
    narrow_gate, narrow_up = (
        (latest_gate / jnp.expand_dims(scale_gate, 1)).astype(jnp.bfloat16),
        (latest_up / jnp.expand_dims(scale_up, 1)).astype(jnp.bfloat16),
    )
    ready_gate, ready_up = (
        lax.all_to_all(narrow_gate, "zero", split_axis=2, concat_axis=1, tiled=True),
        lax.all_to_all(narrow_up, "zero", split_axis=2, concat_axis=1, tiled=True),
    )
    scale_gate = lax.dynamic_slice_in_dim(
        scale_gate, lax.axis_index("zero") * ready_gate.shape[2], ready_gate.shape[2], axis=1
    )
    scale_up = lax.dynamic_slice_in_dim(
        scale_up, lax.axis_index("zero") * ready_up.shape[2], ready_up.shape[2], axis=1
    )
    row_router = lax.all_gather(part_router, "zero", axis=0, tiled=True)
    serve_router = lax.all_gather(row_router, "bank", axis=1, tiled=True)
    return ready_gate, ready_up, scale_gate, scale_up, serve_router


def on_device(n, banks, train_gate, other_gate, train_up, other_up, router_weight, router_gain):
    part_router = (router_weight * router_gain[:, None]).astype(jnp.bfloat16)
    experts, rows, width = train_gate.shape
    held = 2 if experts % 2 == 0 else 1
    whole_tiles = rows % LANES == 0 and width % LANES == 0 and (width // n) % 16 == 0 and part_router.shape[1] % 16 == 0
    staged = 4 * experts * rows * width + SLOTS * held * 12 * rows * width
    weights = (train_gate, other_gate, train_up, other_up, part_router)
    if n > 1 and banks > 1 and whole_tiles and staged <= 48 * 2**20:
        return by_kernel(n, banks, held, *weights)
    return by_collectives(*weights)


def solution(mesh):
    return jax.shard_map(
        functools.partial(on_device, mesh.shape["zero"], mesh.shape["bank"]),
        mesh=mesh,
        in_specs=(
            P("bank", "zero", None),
            P("bank", "zero", None),
            P("bank", "zero", None),
            P("bank", "zero", None),
            P("zero", "bank"),
            P("zero"),
        ),
        out_specs=(
            P("bank", None, "zero"),
            P("bank", None, "zero"),
            P("bank", "zero"),
            P("bank", "zero"),
            P(),
        ),
        check_vma=False,
    )
```

profile of v0, /device:TPU:14, one launch (start us, length us, event | category | flops | bytes accessed | tf_op | source)
XLA Modules:
  0.0 607.9 jit_solution(5629317457525821104)
XLA Ops:
  0.6 1.4 fusion.router
  2.0 584.6 %shard_map.101 = (bf16[32,96,2048]{2,1,0:T(8,128)(2,1)}, bf16[32,96,2048]{2,1,0:T(8,128)(2,1)}, f32[16,2,2,768]{3,2,1,0:T(2,128)}, bf16[128,2048]{1,0:T(8,128)(2,1)}) custom-call(f32[32,256,768]{2,1,0:T(8,128)} %train_gate.1, bf16[32,256,768]{2,1,0:T(8,128)(2,1)} %other_gate.1, f32[32,256,768]{2,1,0:T(8,128)} %train_up.1, bf16[32,256,768]{2,1,0:T(8,128)(2,1)} %other_up.1, ...), custom_call_target="tpu_custom_call" | custom-call | tf_op jit(solution)/shard_map/pallas_call | solution.py:193
  586.6 0.9 dynamic-slice_bitcast_fusion
  587.5 0.6 fusion.1
  588.2 2.0 copy.11
  590.2 0.0 copy-start
  590.2 11.4 %copy.14 = bf16[32,2048,96]{1,2,0:T(8,128)(2,1)} copy(bf16[32,2048,96]{1,2,0:T(8,128)(2,1)} %bitcast.10) | data formatting | bytes 25165824
  601.6 1.5 copy-done
  603.1 4.8 copy.15
Async XLA Ops:
  590.2 12.9 %copy-start = (bf16[32,96,2048]{2,1,0:T(8,128)(2,1)S(1)}, bf16[32,96,2048]{2,1,0:T(8,128)(2,1)}, u32[]{:S(2)}) copy-start(bf16[32,96,2048]{2,1,0:T(8,128)(2,1)} %get-tuple-element.10) | copy-start | bytes 37748740
where the time goes:
time: 608 us
  Pallas kernels  585 us (96%)
  local copies, waits for them, and re-layouts  21.3 us (4%)
    pallas_call x1, Pallas kernels, by_kernel(): pl.pallas_call(functools.partial(exchange, n, banks, held), out_shape=(re...  585 us
    unnamed x5, local copies, waits for them, and re-layouts  19.7 us

commit v1 on v0

v1 whole, which is shorter than its diff:
```python
import functools

import jax
import jax.numpy as jnp
from jax import lax
from jax.experimental import pallas as pl
from jax.experimental.pallas import tpu as pltpu
from jax.sharding import PartitionSpec as P

LANES = 128
MAX_SLOTS = 3
SCALE_SLOTS = 3
DIRECT = 3
OUT_PARTS = 8
VMEM_ALL = 63 * 2**20


def exchange(
    n, banks,
    train_gate, other_gate, train_up, other_up, weight, gain,
    ready_gate, ready_up, scale_ref, serve_router,
    max_train, max_other, train_in, other_in, stage, local_max, direct_in, half_in, half_max, cross_in,
    weight_in, gain_in, part_router, router_row,
    max_sem, in_sem, send_sem, recv_sem, direct_send, direct_recv, half_send, half_recv, cross_send, cross_recv,
    gather_send, gather_recv, row_send, row_recv, bank_send, bank_recv, router_sem,
):
    trains, others, readies = (train_gate, train_up), (other_gate, other_up), (ready_gate, ready_up)
    experts, rows, width = train_gate.shape
    piece = width // n
    half = n // 2
    held = half // 2
    batches = experts // held
    me = lax.axis_index("zero")
    place = lax.rem(me, half)
    first = me - place
    offsets = sorted(range(1, n), key=lambda k: abs(2 * k - n))

    def loads(e, train_to, other_to, sem, slots):
        slot = lax.rem(e, slots)
        out = []
        for t in range(2):
            out.append(pltpu.make_async_copy(trains[t].at[e], train_to.at[slot, t], sem.at[slot, t, 0]))
            out.append(pltpu.make_async_copy(others[t].at[e], other_to.at[slot, t], sem.at[slot, t, 1]))
        return out

    def max_loads(e):
        return loads(e, max_train, max_other, max_sem, MAX_SLOTS)

    def scale_loads(e):
        return loads(e, train_in, other_in, in_sem, SCALE_SLOTS)

    def send(src, dst, send_to, recv_to, **device):
        return pltpu.make_async_remote_copy(
            src_ref=src,
            dst_ref=dst,
            send_sem=send_to,
            recv_sem=recv_to,
            device_id=device,
            device_id_type=pl.DeviceIdType.MESH,
        )

    def await_bytes(ref, sem):
        pltpu.make_async_copy(ref, ref, sem).wait()

    def find_max(e):
        slot = lax.rem(e, MAX_SLOTS)
        for copy in max_loads(e):
            copy.wait()
        for t in range(2):
            for at in range(0, width, LANES):
                cols = pl.ds(at, LANES)
                latest = max_train[slot, t, :, cols] + max_other[slot, t, :, cols].astype(jnp.float32)
                local_max[2 * e + t, :, cols] = jnp.max(jnp.abs(latest), axis=0, keepdims=True)

        @pl.when(e + MAX_SLOTS < experts)
        def _():
            for copy in max_loads(e + MAX_SLOTS):
                copy.start()

    def direct_copy(e, k):
        return send(
            local_max.at[pl.ds(2 * e, 2)], direct_in.at[e, k - 1], direct_send.at[k - 1], direct_recv.at[e],
            zero=lax.rem(me + k, n),
        )

    def find_direct(e):
        find_max(e)
        for k in offsets:
            direct_copy(e, k).start()

    def find_batch(b):
        for i in range(held):
            find_max(b * held + i)
        for k in range(1, half):
            at = lax.rem(place + k, half)
            send(
                local_max.at[b * half + at], half_in.at[b, k - 1], half_send.at[k - 1], half_recv.at[b],
                zero=first + at,
            ).start()

    def cross_batch(b):
        await_bytes(half_in.at[b], half_recv.at[b])
        found = local_max[b * half + place]
        for k in range(half - 1):
            found = jnp.maximum(found, half_in[b, k])
        half_max[b] = found
        send(half_max.at[b], cross_in.at[b], cross_send.at[0], cross_recv.at[b], zero=lax.rem(me + half, n)).start()

    def gather_batch(b):
        await_bytes(cross_in.at[b], cross_recv.at[b])
        row = b * half + place
        scale_ref[row] = jnp.maximum(half_max[b], cross_in[b])
        for k in range(1, half):
            at = lax.rem(place + k, half)
            send(
                scale_ref.at[row], scale_ref.at[row], gather_send.at[k - 1], gather_recv.at[b],
                zero=first + at,
            ).start()

    def mine(ref):
        return ref.at[:, :, pl.ds(pl.multiple_of(me * rows, LANES), rows)]

    def data_copy(t, k, e):
        to = lax.rem(me + k, n)
        return send(
            stage.at[t, pl.ds(e, 1), pl.ds(pl.multiple_of(to * piece, 16), piece), :],
            mine(readies[t]).at[pl.ds(e, 1)],
            send_sem.at[t, k - 1],
            recv_sem.at[t, k - 1],
            zero=to,
        )

    def scale_and_send(e):
        slot = lax.rem(e, SCALE_SLOTS)
        for copy in scale_loads(e):
            copy.wait()
        for t in range(2):
            inverse = 1.0 / scale_ref[2 * e + t]
            for at in range(0, width, LANES):
                cols = pl.ds(at, LANES)
                latest = train_in[slot, t, :, cols] + other_in[slot, t, :, cols].astype(jnp.float32)
                narrow = (latest * inverse[:, at:at + LANES]).astype(jnp.bfloat16)
                stage[t, e, cols, :] = narrow.T
            for k in offsets:
                data_copy(t, k, e).start()
        for t in range(2):
            own = stage[t, e, pl.ds(pl.multiple_of(me * piece, 16), piece), :]
            readies[t][e, :, pl.ds(pl.multiple_of(me * rows, LANES), rows)] = own

        @pl.when(e + SCALE_SLOTS < experts)
        def _():
            for copy in scale_loads(e + SCALE_SLOTS):
                copy.start()

    bank = lax.axis_index("bank")
    parts = weight.shape[0]

    def row_copy(k):
        return send(
            part_router,
            router_row.at[:, pl.ds(pl.multiple_of(me * rows, LANES), rows)],
            row_send.at[k - 1],
            row_recv.at[k - 1],
            zero=lax.rem(me + k, n),
        )

    def bank_copy(k):
        return send(
            router_row,
            serve_router.at[pl.ds(pl.multiple_of(bank * parts, 16), parts)],
            bank_send.at[k - 1],
            bank_recv.at[k - 1],
            bank=lax.rem(bank + k, banks),
        )

    for copy in max_loads(0):
        copy.start()
    barrier = pltpu.get_barrier_semaphore()
    for k in offsets:
        pl.semaphore_signal(
            barrier, inc=1, device_id={"zero": lax.rem(me + k, n)}, device_id_type=pl.DeviceIdType.MESH
        )
    for k in range(1, banks):
        pl.semaphore_signal(
            barrier, inc=1, device_id={"bank": lax.rem(bank + k, banks)}, device_id_type=pl.DeviceIdType.MESH
        )
    for e in range(1, MAX_SLOTS):
        for copy in max_loads(e):
            copy.start()
    router_in = (
        pltpu.make_async_copy(weight, weight_in, router_sem.at[0]),
        pltpu.make_async_copy(gain, gain_in, router_sem.at[1]),
    )
    for copy in router_in:
        copy.start()
    pl.semaphore_wait(barrier, n + banks - 2)
    find_direct(0)
    for e in range(SCALE_SLOTS):
        for copy in scale_loads(e):
            copy.start()

    def direct_step(e, carry):
        find_direct(e)
        return carry

    lax.fori_loop(1, DIRECT * held, direct_step, 0)
    for copy in router_in:
        copy.wait()
    part_router[...] = (weight_in[...] * gain_in[...]).astype(jnp.bfloat16)
    router_row[:, pl.ds(pl.multiple_of(me * rows, LANES), rows)] = part_router[...]
    for k in offsets:
        row_copy(k).start()
    find_batch(DIRECT)

    def step(b, carry):
        @pl.when(b >= DIRECT)
        def _():
            await_bytes(scale_ref.at[pl.ds(b * half, half - 1)], gather_recv.at[b])

        def scale_one(i, carry):
            e = b * held + i

            @pl.when(b < DIRECT)
            def _():
                await_bytes(direct_in.at[e], direct_recv.at[e])
                for t in range(2):
                    found = local_max[2 * e + t]
                    for k in range(n - 1):
                        found = jnp.maximum(found, direct_in[e, k, t])
                    scale_ref[2 * e + t] = found

            scale_and_send(e)
            return carry

        lax.fori_loop(0, held, scale_one, 0)

        @pl.when(jnp.logical_and(b + 2 >= DIRECT, b + 2 < batches))
        def _():
            gather_batch(b + 2)

        @pl.when(b + 3 < batches)
        def _():
            cross_batch(b + 3)

        @pl.when(b + 4 < batches)
        def _():
            find_batch(b + 4)

        return carry

    lax.fori_loop(0, batches, step, 0)

    for k in offsets:
        row_copy(k).wait()
    for k in range(1, banks):
        bank_copy(k).start()
    serve_router[pl.ds(pl.multiple_of(bank * parts, 16), parts), :] = router_row[...]
    for k in range(1, banks):
        bank_copy(k).wait()

    rest = batches - DIRECT
    for k in range(1, half):
        await_bytes(local_max.at[pl.ds(0, rest)], half_send.at[k - 1])
        await_bytes(local_max.at[pl.ds(0, rest)], gather_send.at[k - 1])
    await_bytes(local_max.at[pl.ds(0, rest)], cross_send.at[0])
    for k in offsets:
        await_bytes(local_max.at[pl.ds(0, DIRECT * half)], direct_send.at[k - 1])
        to, source = lax.rem(me + k, n), lax.rem(me + n - k, n)
        for t in range(2):
            await_bytes(stage.at[t, :, pl.ds(pl.multiple_of(to * piece, 16), piece), :], send_sem.at[t, k - 1])
            got = readies[t].at[:, :, pl.ds(pl.multiple_of(source * rows, LANES), rows)]
            await_bytes(got, recv_sem.at[t, k - 1])


def finish(
    n, ready_gate, ready_up, scales, router, out_gate, out_up, scale_gate, scale_up, serve_router, turned, sem, small_sem
):
    experts, piece, _ = ready_gate.shape
    me = lax.axis_index("zero")
    count = experts // OUT_PARTS if experts % OUT_PARTS == 0 else experts
    copies = []
    for at in range(0, experts, count):
        for t, (ready, out) in enumerate(((ready_gate, out_gate), (ready_up, out_up))):
            copies.append(pltpu.make_async_copy(ready.at[pl.ds(at, count)], out.at[pl.ds(at, count)], sem.at[t, at // count]))
    for copy in copies:
        copy.start()
    turned[...] = router[...].T
    copies.append(pltpu.make_async_copy(turned, serve_router, small_sem.at[0]))
    copies[-1].start()
    for k in range(n):

        @pl.when(me == k)
        def _():
            scale_gate[...] = scales[:, 0, 0, k * piece:(k + 1) * piece]
            scale_up[...] = scales[:, 1, 0, k * piece:(k + 1) * piece]

    for copy in copies:
        copy.wait()


def by_kernel(n, banks, train_gate, other_gate, train_up, other_up, router_weight, router_gain):
    experts, rows, width = train_gate.shape
    piece = width // n
    parts = router_weight.shape[1]
    anywhere = pl.BlockSpec(memory_space=pltpu.MemorySpace.HBM)
    inside = pl.BlockSpec(memory_space=pltpu.MemorySpace.VMEM)
    ready = pltpu.VMEM((experts, piece, n * rows), jnp.bfloat16)
    half = n // 2
    batches = 2 * experts // half
    outs = (
        ready,
        ready,
        pltpu.VMEM((2 * experts, 1, width), jnp.float32),
        pltpu.VMEM((banks * parts, n * rows), jnp.bfloat16),
    )
    dma = pltpu.SemaphoreType.DMA
    ready_gate, ready_up, scales, router = pl.pallas_call(
        functools.partial(exchange, n, banks),
        out_shape=outs,
        in_specs=[anywhere] * 6,
        out_specs=(inside,) * 4,
        scratch_shapes=[
            pltpu.VMEM((MAX_SLOTS, 2, rows, width), jnp.float32),
            pltpu.VMEM((MAX_SLOTS, 2, rows, width), jnp.bfloat16),
            pltpu.VMEM((SCALE_SLOTS, 2, rows, width), jnp.float32),
            pltpu.VMEM((SCALE_SLOTS, 2, rows, width), jnp.bfloat16),
            pltpu.VMEM((2, experts, width, rows), jnp.bfloat16),
            pltpu.VMEM((2 * experts, 1, width), jnp.float32),
            pltpu.VMEM((DIRECT * half // 2, n - 1, 2, 1, width), jnp.float32),
            pltpu.VMEM((batches, half - 1, 1, width), jnp.float32),
            pltpu.VMEM((batches, 1, width), jnp.float32),
            pltpu.VMEM((batches, 1, width), jnp.float32),
            pltpu.VMEM((parts, rows), jnp.float32),
            pltpu.VMEM((1, rows), jnp.float32),
            pltpu.VMEM((parts, rows), jnp.bfloat16),
            pltpu.VMEM((parts, n * rows), jnp.bfloat16),
            dma((MAX_SLOTS, 2, 2)),
            dma((SCALE_SLOTS, 2, 2)),
            dma((2, n - 1)),
            dma((2, n - 1)),
            dma((n - 1,)),
            dma((DIRECT * half // 2,)),
            dma((half - 1,)),
            dma((batches,)),
            dma((1,)),
            dma((batches,)),
            dma((half - 1,)),
            dma((batches,)),
            dma((n - 1,)),
            dma((n - 1,)),
            dma((banks - 1,)),
            dma((banks - 1,)),
            dma((2,)),
        ],
        compiler_params=pltpu.CompilerParams(
            collective_id=0, has_side_effects=True, vmem_limit_bytes=39 * 2**20
        ),
    )(train_gate, other_gate, train_up, other_up, router_weight.T, router_gain.reshape(1, rows))
    scales = scales.reshape(experts, 2, 1, width)
    out = jax.ShapeDtypeStruct((experts, piece, n * rows), jnp.bfloat16)
    scale = jax.ShapeDtypeStruct((experts, piece), jnp.float32)
    out_gate, out_up, scale_gate, scale_up, serve_router = pl.pallas_call(
        functools.partial(finish, n),
        out_shape=(out, out, scale, scale, jax.ShapeDtypeStruct((n * rows, banks * parts), jnp.bfloat16)),
        in_specs=[inside] * 4,
        out_specs=(anywhere, anywhere, inside, inside, anywhere),
        scratch_shapes=[
            pltpu.VMEM((n * rows, banks * parts), jnp.bfloat16),
            pltpu.SemaphoreType.DMA((2, OUT_PARTS)),
            pltpu.SemaphoreType.DMA((1,)),
        ],
        compiler_params=pltpu.CompilerParams(vmem_limit_bytes=4 * 2**20),
    )(ready_gate, ready_up, scales, router)
    return jnp.swapaxes(out_gate, 1, 2), jnp.swapaxes(out_up, 1, 2), scale_gate, scale_up, serve_router


def by_collectives(train_gate, other_gate, train_up, other_up, part_router):
    latest_gate = train_gate + other_gate.astype(jnp.float32)
    latest_up = train_up + other_up.astype(jnp.float32)
    scale_gate, scale_up = lax.pmax(
        (jnp.max(jnp.abs(latest_gate), axis=1), jnp.max(jnp.abs(latest_up), axis=1)), "zero"
    )
    narrow_gate, narrow_up = (
        (latest_gate / jnp.expand_dims(scale_gate, 1)).astype(jnp.bfloat16),
        (latest_up / jnp.expand_dims(scale_up, 1)).astype(jnp.bfloat16),
    )
    ready_gate, ready_up = (
        lax.all_to_all(narrow_gate, "zero", split_axis=2, concat_axis=1, tiled=True),
        lax.all_to_all(narrow_up, "zero", split_axis=2, concat_axis=1, tiled=True),
    )
    scale_gate = lax.dynamic_slice_in_dim(
        scale_gate, lax.axis_index("zero") * ready_gate.shape[2], ready_gate.shape[2], axis=1
    )
    scale_up = lax.dynamic_slice_in_dim(
        scale_up, lax.axis_index("zero") * ready_up.shape[2], ready_up.shape[2], axis=1
    )
    row_router = lax.all_gather(part_router, "zero", axis=0, tiled=True)
    serve_router = lax.all_gather(row_router, "bank", axis=1, tiled=True)
    return ready_gate, ready_up, scale_gate, scale_up, serve_router


def on_device(n, banks, train_gate, other_gate, train_up, other_up, router_weight, router_gain):
    experts, rows, width = train_gate.shape
    weights = (train_gate, other_gate, train_up, other_up)
    whole_tiles = rows % LANES == 0 and width % LANES == 0 and (width // n) % 16 == 0
    even_parts = n % 4 == 0 and experts % (n // 4) == 0 and router_weight.shape[1] % 16 == 0
    held = 8 * experts * rows * width + (MAX_SLOTS + SCALE_SLOTS) * 12 * rows * width
    held += 4 * width * (8 * experts + DIRECT * n * n)
    if banks > 1 and whole_tiles and even_parts and experts >= 2 * n and held <= VMEM_ALL:
        return by_kernel(n, banks, *weights, router_weight, router_gain)
    return by_collectives(*weights, (router_weight * router_gain[:, None]).astype(jnp.bfloat16))


def solution(mesh):
    return jax.shard_map(
        functools.partial(on_device, mesh.shape["zero"], mesh.shape["bank"]),
        mesh=mesh,
        in_specs=(
            P("bank", "zero", None),
            P("bank", "zero", None),
            P("bank", "zero", None),
            P("bank", "zero", None),
            P("zero", "bank"),
            P("zero"),
        ),
        out_specs=(
            P("bank", None, "zero"),
            P("bank", None, "zero"),
            P("bank", "zero"),
            P("bank", "zero"),
            P(),
        ),
        check_vma=False,
    )
```

time: 608 us -> 569 us (0.936)
  local copies, waits for them, and re-layouts: 21.3 us -> 0 us
  Pallas kernels: 585 us -> 566 us
    unnamed x5 -> x0, local copies, waits for them, and re-layouts: 19.7 us -> none
    pallas_call x1 -> x2, Pallas kernels: 585 us -> 566 us  [the longest x1 557 us: by_kernel(): pl.pallas_call(functools.partial(exchange, n, banks), out_shape=outs, in_...]
where the time goes in v1:
time: 569 us; the launch traced here: 567 us
  Pallas kernels  566 us (99%)
    pallas_call x1, Pallas kernels, by_kernel(): pl.pallas_call(functools.partial(exchange, n, banks), out_shape=outs, in_...  557 us

profile of v1, /device:TPU:14, one launch (start us, length us, event | category | flops | bytes accessed | tf_op | source)
XLA Modules:
  0.0 566.9 jit_solution(9127346287917416552)
XLA Ops:
  0.6 557.0 %shard_map.101 = (bf16[32,96,2048]{2,1,0:T(8,128)(2,1)S(1)}, bf16[32,96,2048]{2,1,0:T(8,128)(2,1)S(1)}, f32[64,1,768]{2,1,0:T(1,128)S(1)}, bf16[128,2048]{1,0:T(8,128)(2,1)S(1)}) custom-call(f32[32,256,768]{2,1,0:T(8,128)} %train_gate.1, bf16[32,256,768]{2,1,0:T(8,128)(2,1)} %other_gate.1, f32[32,256,768]{2,1,0:T(8,128)} %train_up.1, ...), custom_call_target="tpu_custom_call" | custom-call | tf_op jit(solution)/shard_map/pallas_call | solution.py:317
  557.6 9.3 %shard_map.102 = (bf16[32,96,2048]{2,1,0:T(8,128)(2,1)}, bf16[32,96,2048]{2,1,0:T(8,128)(2,1)}, f32[32,96]{1,0:T(8,128)}, f32[32,96]{1,0:T(8,128)}, bf16[2048,128]{1,0:T(8,128)(2,1)}) custom-call(bf16[32,96,2048]{2,1,0:T(8,128)(2,1)S(1)} %get-tuple-element.14.ready_gate, bf16[32,96,2048]{2,1,0:T(8,128)(2,1)S(1)} %get-tuple-element.15.ready_up, ...), custom_call_target="tpu_custom_call" | custom-call | tf_op jit(solution)/shard_map/pallas_call | solution.py:362

commit v2 on v1

--- a/solution.py
+++ b/solution.py
@@ -10,7 +10,6 @@
 LANES = 128
 MAX_SLOTS = 3
 SCALE_SLOTS = 3
-DIRECT = 3
 OUT_PARTS = 8
 VMEM_ALL = 63 * 2**20
 
@@ -64,9 +63,10 @@
 
     def find_max(e):
         slot = lax.rem(e, MAX_SLOTS)
-        for copy in max_loads(e):
-            copy.wait()
+        copies = max_loads(e)
         for t in range(2):
+            for copy in copies[2 * t:2 * t + 2]:
+                copy.wait()
             for at in range(0, width, LANES):
                 cols = pl.ds(at, LANES)
                 latest = max_train[slot, t, :, cols] + max_other[slot, t, :, cols].astype(jnp.float32)
@@ -83,8 +83,7 @@
             zero=lax.rem(me + k, n),
         )
 
-    def find_direct(e):
-        find_max(e)
+    def send_direct(e):
         for k in offsets:
             direct_copy(e, k).start()
 
@@ -120,11 +119,11 @@
     def mine(ref):
         return ref.at[:, :, pl.ds(pl.multiple_of(me * rows, LANES), rows)]
 
-    def data_copy(t, k, e):
+    def data_copy(t, k, some):
         to = lax.rem(me + k, n)
         return send(
-            stage.at[t, pl.ds(e, 1), pl.ds(pl.multiple_of(to * piece, 16), piece), :],
-            mine(readies[t]).at[pl.ds(e, 1)],
+            stage.at[t, some, pl.ds(pl.multiple_of(to * piece, 16), piece), :],
+            mine(readies[t]).at[some],
             send_sem.at[t, k - 1],
             recv_sem.at[t, k - 1],
             zero=to,
@@ -132,17 +131,27 @@
 
     def scale_and_send(e):
         slot = lax.rem(e, SCALE_SLOTS)
-        for copy in scale_loads(e):
-            copy.wait()
+        copies = scale_loads(e)
         for t in range(2):
+            for copy in copies[2 * t:2 * t + 2]:
+                copy.wait()
             inverse = 1.0 / scale_ref[2 * e + t]
             for at in range(0, width, LANES):
                 cols = pl.ds(at, LANES)
                 latest = train_in[slot, t, :, cols] + other_in[slot, t, :, cols].astype(jnp.float32)
                 narrow = (latest * inverse[:, at:at + LANES]).astype(jnp.bfloat16)
                 stage[t, e, cols, :] = narrow.T
-            for k in offsets:
-                data_copy(t, k, e).start()
+
+            @pl.when(e < held)
+            def _():
+                for k in offsets:
+                    data_copy(t, k, pl.ds(e, 1)).start()
+
+            @pl.when(jnp.logical_and(e >= held, lax.rem(e, held) == held - 1))
+            def _():
+                for k in offsets:
+                    data_copy(t, k, pl.ds(e - held + 1, held)).start()
+
         for t in range(2):
             own = stage[t, e, pl.ds(pl.multiple_of(me * piece, 16), piece), :]
             readies[t][e, :, pl.ds(pl.multiple_of(me * rows, LANES), rows)] = own
@@ -155,14 +164,25 @@
     bank = lax.axis_index("bank")
     parts = weight.shape[0]
 
-    def row_copy(k):
-        return send(
-            part_router,
-            router_row.at[:, pl.ds(pl.multiple_of(me * rows, LANES), rows)],
-            row_send.at[k - 1],
-            row_recv.at[k - 1],
-            zero=lax.rem(me + k, n),
-        )
+    partner = lax.rem(me + half, n)
+
+    def row_block(ref, owner):
+        return ref.at[:, pl.ds(pl.multiple_of(owner * rows, LANES), rows)]
+
+    def row_copies():
+        out = []
+        for k in range(1, half + 1):
+            to = partner if k == half else first + lax.rem(place + k, half)
+            out.append(send(part_router, row_block(router_row, me), row_send.at[k - 1], row_recv.at[k - 1], zero=to))
+        return out
+
+    def pass_on_copies():
+        block = row_block(router_row, partner)
+        out = []
+        for k in range(1, half):
+            to = first + lax.rem(place + k, half)
+            out.append(send(block, block, row_send.at[half + k - 1], row_recv.at[half + k - 1], zero=to))
+        return out
 
     def bank_copy(k):
         return send(
@@ -184,57 +204,68 @@
         pl.semaphore_signal(
             barrier, inc=1, device_id={"bank": lax.rem(bank + k, banks)}, device_id_type=pl.DeviceIdType.MESH
         )
+    router_in = (
+        pltpu.make_async_copy(weight, weight_in, router_sem.at[0]),
+        pltpu.make_async_copy(gain, gain_in, router_sem.at[1]),
+    )
+    for copy in router_in:
+        copy.start()
+    find_max(0)
+    pl.semaphore_wait(barrier, n + banks - 2)
+    send_direct(0)
     for e in range(1, MAX_SLOTS):
         for copy in max_loads(e):
             copy.start()
-    router_in = (
-        pltpu.make_async_copy(weight, weight_in, router_sem.at[0]),
-        pltpu.make_async_copy(gain, gain_in, router_sem.at[1]),
-    )
-    for copy in router_in:
+    for copy in scale_loads(0):
         copy.start()
-    pl.semaphore_wait(barrier, n + banks - 2)
-    find_direct(0)
-    for e in range(SCALE_SLOTS):
-        for copy in scale_loads(e):
-            copy.start()
-
-    def direct_step(e, carry):
-        find_direct(e)
-        return carry
-
-    lax.fori_loop(1, DIRECT * held, direct_step, 0)
     for copy in router_in:
         copy.wait()
     part_router[...] = (weight_in[...] * gain_in[...]).astype(jnp.bfloat16)
-    router_row[:, pl.ds(pl.multiple_of(me * rows, LANES), rows)] = part_router[...]
-    for k in offsets:
-        row_copy(k).start()
-    find_batch(DIRECT)
+    row_block(router_row, me)[...] = part_router[...]
+    for e in range(1, held):
+        find_max(e)
+        send_direct(e)
+    for copy in row_copies():
+        copy.start()
+    for e in range(1, SCALE_SLOTS):
+        for copy in scale_loads(e):
+            copy.start()
+
+    def scale_one(e, carry):
+        @pl.when(e < held)
+        def _():
+            await_bytes(direct_in.at[e], direct_recv.at[e])
+            for t in range(2):
+                found = local_max[2 * e + t]
+                for k in range(n - 1):
+                    found = jnp.maximum(found, direct_in[e, k, t])
+                scale_ref[2 * e + t] = found
+
+        scale_and_send(e)
+        return carry
+
+    find_batch(1)
+    find_batch(2)
+    cross_batch(1)
+    scale_one(0, 0)
+    find_batch(3)
+    gather_batch(1)
+    cross_batch(2)
 
     def step(b, carry):
-        @pl.when(b >= DIRECT)
+        @pl.when(b >= 1)
         def _():
             await_bytes(scale_ref.at[pl.ds(b * half, half - 1)], gather_recv.at[b])
 
-        def scale_one(i, carry):
-            e = b * held + i
-
-            @pl.when(b < DIRECT)
-            def _():
-                await_bytes(direct_in.at[e], direct_recv.at[e])
-                for t in range(2):
-                    found = local_max[2 * e + t]
-                    for k in range(n - 1):
-                        found = jnp.maximum(found, direct_in[e, k, t])
-                    scale_ref[2 * e + t] = found
-
-            scale_and_send(e)
-            return carry
-
-        lax.fori_loop(0, held, scale_one, 0)
-
-        @pl.when(jnp.logical_and(b + 2 >= DIRECT, b + 2 < batches))
+        lax.fori_loop(jnp.maximum(b * held, 1), (b + 1) * held, scale_one, 0)
+
+        @pl.when(b == 2)
+        def _():
+            row_copies()[half - 1].wait_recv()
+            for copy in pass_on_copies():
+                copy.start()
+
+        @pl.when(b + 2 < batches)
         def _():
             gather_batch(b + 2)
 
@@ -250,21 +281,23 @@
 
     lax.fori_loop(0, batches, step, 0)
 
-    for k in offsets:
-        row_copy(k).wait()
+    rows_in = row_copies()
+    for copy in rows_in[:half - 1] + pass_on_copies():
+        copy.wait()
+    rows_in[half - 1].wait_send()
     for k in range(1, banks):
         bank_copy(k).start()
     serve_router[pl.ds(pl.multiple_of(bank * parts, 16), parts), :] = router_row[...]
     for k in range(1, banks):
         bank_copy(k).wait()
 
-    rest = batches - DIRECT
+    rest = batches - 1
     for k in range(1, half):
         await_bytes(local_max.at[pl.ds(0, rest)], half_send.at[k - 1])
         await_bytes(local_max.at[pl.ds(0, rest)], gather_send.at[k - 1])
     await_bytes(local_max.at[pl.ds(0, rest)], cross_send.at[0])
     for k in offsets:
-        await_bytes(local_max.at[pl.ds(0, DIRECT * half)], direct_send.at[k - 1])
+        await_bytes(local_max.at[pl.ds(0, half)], direct_send.at[k - 1])
         to, source = lax.rem(me + k, n), lax.rem(me + n - k, n)
         for t in range(2):
             await_bytes(stage.at[t, :, pl.ds(pl.multiple_of(to * piece, 16), piece), :], send_sem.at[t, k - 1])
@@ -273,20 +306,20 @@
 
 
 def finish(
-    n, ready_gate, ready_up, scales, router, out_gate, out_up, scale_gate, scale_up, serve_router, turned, sem, small_sem
+    n, ready_gate, ready_up, scales, router, out_gate, out_up, out_scale_gate, out_scale_up, serve_router,
+    scale_gate, scale_up, turned, sem, small_sem,
 ):
     experts, piece, _ = ready_gate.shape
     me = lax.axis_index("zero")
-    count = experts // OUT_PARTS if experts % OUT_PARTS == 0 else experts
+    count = experts // OUT_PARTS
     copies = []
-    for at in range(0, experts, count):
+    for i in range(OUT_PARTS):
+        some = pl.ds(i * count, count)
         for t, (ready, out) in enumerate(((ready_gate, out_gate), (ready_up, out_up))):
-            copies.append(pltpu.make_async_copy(ready.at[pl.ds(at, count)], out.at[pl.ds(at, count)], sem.at[t, at // count]))
+            copies.append(pltpu.make_async_copy(ready.at[some], out.at[some], sem.at[t, i]))
     for copy in copies:
         copy.start()
     turned[...] = router[...].T
-    copies.append(pltpu.make_async_copy(turned, serve_router, small_sem.at[0]))
-    copies[-1].start()
     for k in range(n):
 
         @pl.when(me == k)
@@ -294,6 +327,10 @@
             scale_gate[...] = scales[:, 0, 0, k * piece:(k + 1) * piece]
             scale_up[...] = scales[:, 1, 0, k * piece:(k + 1) * piece]
 
+    small = ((turned, serve_router), (scale_gate, out_scale_gate), (scale_up, out_scale_up))
+    for i, (source, target) in enumerate(small):
+        copies.append(pltpu.make_async_copy(source, target, small_sem.at[i]))
+        copies[-1].start()
     for copy in copies:
         copy.wait()
 
@@ -326,7 +363,7 @@
             pltpu.VMEM((SCALE_SLOTS, 2, rows, width), jnp.bfloat16),
             pltpu.VMEM((2, experts, width, rows), jnp.bfloat16),
             pltpu.VMEM((2 * experts, 1, width), jnp.float32),
-            pltpu.VMEM((DIRECT * half // 2, n - 1, 2, 1, width), jnp.float32),
+            pltpu.VMEM((half // 2, n - 1, 2, 1, width), jnp.float32),
             pltpu.VMEM((batches, half - 1, 1, width), jnp.float32),
             pltpu.VMEM((batches, 1, width), jnp.float32),
             pltpu.VMEM((batches, 1, width), jnp.float32),
@@ -339,7 +376,7 @@
             dma((2, n - 1)),
             dma((2, n - 1)),
             dma((n - 1,)),
-            dma((DIRECT * half // 2,)),
+            dma((half // 2,)),
             dma((half - 1,)),
             dma((batches,)),
             dma((1,)),
@@ -363,11 +400,13 @@
         functools.partial(finish, n),
         out_shape=(out, out, scale, scale, jax.ShapeDtypeStruct((n * rows, banks * parts), jnp.bfloat16)),
         in_specs=[inside] * 4,
-        out_specs=(anywhere, anywhere, inside, inside, anywhere),
+        out_specs=(anywhere,) * 5,
         scratch_shapes=[
+            pltpu.VMEM((experts, piece), jnp.float32),
+            pltpu.VMEM((experts, piece), jnp.float32),
             pltpu.VMEM((n * rows, banks * parts), jnp.bfloat16),
             pltpu.SemaphoreType.DMA((2, OUT_PARTS)),
-            pltpu.SemaphoreType.DMA((1,)),
+            pltpu.SemaphoreType.DMA((3,)),
         ],
         compiler_params=pltpu.CompilerParams(vmem_limit_bytes=4 * 2**20),
     )(ready_gate, ready_up, scales, router)
@@ -405,8 +444,8 @@
     whole_tiles = rows % LANES == 0 and width % LANES == 0 and (width // n) % 16 == 0
     even_parts = n % 4 == 0 and experts % (n // 4) == 0 and router_weight.shape[1] % 16 == 0
     held = 8 * experts * rows * width + (MAX_SLOTS + SCALE_SLOTS) * 12 * rows * width
-    held += 4 * width * (8 * experts + DIRECT * n * n)
-    if banks > 1 and whole_tiles and even_parts and experts >= 2 * n and held <= VMEM_ALL:
+    held += 4 * width * (8 * experts + n * n)
+    if banks > 1 and whole_tiles and even_parts and experts >= 2 * n and experts % OUT_PARTS == 0 and held <= VMEM_ALL:
         return by_kernel(n, banks, *weights, router_weight, router_gain)
     return by_collectives(*weights, (router_weight * router_gain[:, None]).astype(jnp.bfloat16))
 

time: 569 us -> 564 us (level)
  no operation moved by 1% of the time
where the time goes in v2:
time: 564 us
  Pallas kernels  563 us (100%)
    pallas_call x1, Pallas kernels, by_kernel(): pl.pallas_call(functools.partial(exchange, n, banks), out_shape=outs, in_...  555 us

profile of v2, /device:TPU:14, one launch (start us, length us, event | category | flops | bytes accessed | tf_op | source)
XLA Modules:
  0.0 564.0 jit_solution(2566784762288276881)
XLA Ops:
  0.6 554.7 %shard_map.101 = (bf16[32,96,2048]{2,1,0:T(8,128)(2,1)S(1)}, bf16[32,96,2048]{2,1,0:T(8,128)(2,1)S(1)}, f32[64,1,768]{2,1,0:T(1,128)S(1)}, bf16[128,2048]{1,0:T(8,128)(2,1)S(1)}) custom-call(f32[32,256,768]{2,1,0:T(8,128)} %train_gate.1, bf16[32,256,768]{2,1,0:T(8,128)(2,1)} %other_gate.1, f32[32,256,768]{2,1,0:T(8,128)} %train_up.1, ...), custom_call_target="tpu_custom_call" | custom-call | tf_op jit(solution)/shard_map/pallas_call | solution.py:354
  555.3 8.7 %shard_map.102 = (bf16[32,96,2048]{2,1,0:T(8,128)(2,1)}, bf16[32,96,2048]{2,1,0:T(8,128)(2,1)}, f32[32,96]{1,0:T(8,128)}, f32[32,96]{1,0:T(8,128)}, bf16[2048,128]{1,0:T(8,128)(2,1)}) custom-call(bf16[32,96,2048]{2,1,0:T(8,128)(2,1)S(1)} %get-tuple-element.14.ready_gate, bf16[32,96,2048]{2,1,0:T(8,128)(2,1)S(1)} %get-tuple-element.15.ready_up, ...), custom_call_target="tpu_custom_call" | custom-call | tf_op jit(solution)/shard_map/pallas_call | solution.py:399
